TPU v7x, 32 devices: a whole 2x2x4 slice. The times are simulated.
32 devices in a mesh: row: 8 (over y, x, core), col: 4 (over z).
Axes of the slice: x: 2, y: 2, z: 4, core: 2. Of those that a mesh axis runs over, the one named last changes fastest.
Arguments:
- state: float32 [9, 35, 8192], P(None, None, ('col', 'row')), may hold values from -6 to 6
- geometry: bfloat16 [9, 128, 8192], P(None, 'row', 'col'), may hold values from -5 to 5
- material: float32 [4, 8192], P(None, ('col', 'row')), may hold values from 0.5 to 2
- neighbours: int32 [4, 4, 8192], P(None, None, ('col', 'row')), may hold values from 0 to 1023, as said below
- send_faces: int32 [32, 4, 64], P(('col', 'row')), may hold values from 0 to 1023, as said below
- vol_eval: float32 [35, 128], replicated, may hold values from -1 to 1
- vol_grad: bfloat16 [3, 35, 128], replicated, may hold values from -0.3125 to 0.3125
- face_eval: float32 [4, 35, 27], replicated, may hold values from -1 to 1
- face_lift: float32 [4, 35, 27], replicated, may hold values from -0.625 to 0.625
- normals: bfloat16 [3, 27, 4, 8192], P(None, None, None, ('col', 'row')), may hold values from -5 to 5
- areas: float32 [27, 4, 8192], P(None, None, ('col', 'row')), may hold values from 0.5 to 2
Outputs:
- section: float32 [9, 35, 8192], P(None, None, ('col', 'row'))
Inputs may be any that keep to these rules, and one draw needn't show every extreme that they name: `neighbours`: field 0 is the kind: 0 the neighbour face lies in the same block, 1 in another block of the same row group, 2 free surface, 3 absorbing. Field 1 is the neighbour block's col index (the own col index for kinds 0, 2, 3). Field 2 is, for kind 0, the neighbour's face number f * 256 + e within the block; for kind 1, a slot below the number of faces that the neighbour's block lists for this block in send_faces; else 0. Field 3 is an orientation of 0 to 2 (0 for kinds 2 and 3). Neighbouring is mutual: the neighbour face names this face back, with orientation (3 - turn) % 3. `send_faces`: A block lists at most 64 faces for one col index, the same number as that block lists back, and nothing for its own col index; entries past the count are 0. In every row group some pair of blocks lists exactly 64 faces to each other.
All inputs are finite; a program needn't handle non-finite values.
Results may differ from a plain program's by a relative error of at most 0.0065.
Values may be sent and summed in bfloat16 or wider, within the bound.
A program may use at most 64 MiB of HBM per device.

v0:
```python
import functools

import jax
import jax.numpy as jnp
from jax import lax
from jax.experimental import pallas as pl
from jax.experimental.pallas import tpu as pltpu
from jax.sharding import PartitionSpec as P

F32 = jnp.float32
BF16 = jnp.bfloat16
QP = 32
MESH = pl.DeviceIdType.MESH


def dot(left, right, left_dim=1, right_dim=0):
    return lax.dot_general(
        left, right, (((left_dim,), (right_dim,)), ((), ())), preferred_element_type=F32
    )


def partner(row, step, rows):
    if rows & (rows - 1):
        other = row - step
        return other + jnp.where(other < 0, rows, 0)
    total, bit = 0, 1
    while bit < rows:
        total = total + ((row // bit + step // bit) % 2) * bit
        bit *= 2
    return total


def one_hot(shape, hit):
    row_id = lax.broadcasted_iota(jnp.int32, shape, 0)
    col_id = lax.broadcasted_iota(jnp.int32, shape, 1)
    return jnp.where(hit(row_id, col_id), 1.0, 0.0).astype(BF16)


def kernel(
    rows,
    cols,
    state_in,
    geometry,
    material_in,
    neighbours_in,
    send_in,
    vol_eval_in,
    vol_grad_in,
    face_eval_in,
    face_lift_in,
    normals_in,
    areas_in,
    out,
    state,
    material,
    neighbours,
    send_faces,
    vol_eval,
    vol_grad,
    face_eval,
    face_lift,
    normals,
    areas,
    metric,
    state_low,
    traces,
    turned,
    outgoing,
    pool,
    gathered,
    points,
    fluxes,
    tests,
    normal_rows,
    area_rows,
    pick,
    far,
    load_sem,
    geo_send,
    geo_recv,
    face_send,
    face_recv,
    metric_by_row=None,
):
    row = lax.axis_index("row")
    col = lax.axis_index("col")
    quantities, basis, elems = state.shape
    local_q = geometry.shape[1]
    vol_q = vol_eval.shape[1]
    face_q = face_eval.shape[0]
    slots = send_faces.shape[2]
    direct = local_q % 16 == 0
    unit = local_q if direct else 16
    span = vol_q // 2
    tile = 3 * span + 2 * QP
    paired = rows & (rows - 1) == 0

    barrier = pltpu.get_barrier_semaphore()
    for step in range(1, rows):
        pl.semaphore_signal(
            barrier, inc=1, device_id={"row": lax.rem(row + step, rows)}, device_id_type=MESH
        )
    for step in range(1, cols):
        pl.semaphore_signal(
            barrier, inc=1, device_id={"col": lax.rem(col + step, cols)}, device_id_type=MESH
        )
    loads = {}
    pairs = [
        ("state", state_in, state),
        ("face_eval", face_eval_in, face_eval),
        ("material", material_in, material),
        ("neighbours", neighbours_in, neighbours),
        ("send_faces", send_in, send_faces),
        ("vol_eval", vol_eval_in, vol_eval),
        ("normals", normals_in, normals),
        ("areas", areas_in, areas),
        ("vol_grad", vol_grad_in, vol_grad),
        ("face_lift", face_lift_in, face_lift),
    ]
    for index, (name, source, target) in enumerate(pairs):
        loads[name] = pltpu.make_async_copy(source, target, load_sem.at[index])
        loads[name].start()
    own_copy = pltpu.make_async_copy(
        geometry.at[:, :, pl.ds(pl.multiple_of(row * elems, 128), elems)],
        metric.at[0],
        geo_recv.at[0],
    )
    own_copy.start()
    pl.semaphore_wait(barrier, rows + cols - 2)

    geo_copies = [own_copy]
    for step in range(1, rows):
        peer = partner(row, step, rows) if paired else lax.rem(row + step, rows)
        copy = pltpu.make_async_remote_copy(
            src_ref=geometry.at[:, :, pl.ds(pl.multiple_of(peer * elems, 128), elems)],
            dst_ref=metric.at[step],
            send_sem=geo_send.at[step],
            recv_sem=geo_recv.at[step],
            device_id={"row": peer},
            device_id_type=MESH,
        )
        copy.start()
        geo_copies.append(copy)

    pool[col] = jnp.zeros((slots, quantities * QP), BF16)
    loads["face_eval"].wait()

    def turning_rows(r, c):
        f = r // (3 * QP)
        turn_id = r // QP - 3 * f
        q = r % QP
        k = q % 3
        moved = k + turn_id
        moved = jnp.where(moved >= 3, moved - 3, moved)
        return (c == (q - k + moved) * 4 + f) & (q < face_q)

    turning = one_hot((12 * QP, 4 * face_q), turning_rows)
    flat = face_eval[...].reshape(4 * face_q, basis).astype(BF16)
    face_basis = dot(turning, flat).astype(BF16)
    loads["state"].wait()
    for m in range(quantities):
        state_low[m] = state[m].astype(BF16)
    loads["material"].wait()
    loads["neighbours"].wait()
    kind = neighbours[0]
    peer_index = neighbours[1]
    target = neighbours[2]
    turn = neighbours[3]
    row_ids = lax.broadcasted_iota(jnp.int32, (QP, elems), 0)
    low_rows = []
    for i in range(3):
        low_rows.append(material[i : i + 1, :].astype(BF16).astype(F32))
    for i in range(3):
        low_rows.append(material[i : i + 1, :] - low_rows[i])

    for m in range(quantities):
        found = dot(face_basis, state_low[m])
        for f in range(4):
            zero = found[3 * f * QP : (3 * f + 1) * QP]
            one = found[(3 * f + 1) * QP : (3 * f + 2) * QP]
            two = found[(3 * f + 2) * QP : (3 * f + 3) * QP]
            traces[m, f * QP : (f + 1) * QP, :] = zero
            side = turn[f : f + 1]
            chosen = jnp.where(side == 0, zero, jnp.where(side == 1, two, one))
            if m < 6:
                chosen = jnp.where(row_ids == face_q, low_rows[m], chosen)
            turned[m * QP : (m + 1) * QP, f * elems : (f + 1) * elems] = chosen.astype(BF16)

    loads["send_faces"].wait()
    same = one_hot((slots, slots), lambda r, c: r == c)
    listed = send_faces[0]
    listed_face = listed // elems
    listed_elem = listed - listed_face * elems
    face_col = dot(same, listed_face.astype(F32).astype(BF16), 1, 1)
    elem_col = dot(same, listed_elem.astype(F32).astype(BF16), 1, 1)
    listed_col = (face_col * float(elems) + elem_col).astype(jnp.int32)
    face_ids = lax.broadcasted_iota(jnp.int32, (slots, 4 * elems), 1)
    send_pick = jnp.concatenate(
        [
            jnp.where(face_ids == listed_col[:, p : p + 1], 1.0, 0.0).astype(BF16)
            for p in range(cols)
        ],
        axis=0,
    )
    listed_traces = dot(send_pick, turned[...], 1, 1).astype(BF16)
    for p in range(cols):
        outgoing[p] = listed_traces[p * slots : (p + 1) * slots]

    face_copies = []
    for step in range(1, cols):
        peer = lax.rem(col + step, cols)
        copy = pltpu.make_async_remote_copy(
            src_ref=outgoing.at[peer],
            dst_ref=pool.at[col],
            send_sem=face_send.at[step],
            recv_sem=face_recv.at[step],
            device_id={"col": peer},
            device_id_type=MESH,
        )
        copy.start()
        face_copies.append(copy)

    loads["vol_eval"].wait()
    same_q = one_hot((vol_q, vol_q), lambda r, c: r == c)
    vol_basis = dot(same_q, vol_eval[...].astype(BF16), 1, 1).astype(BF16)
    for m in range(quantities):
        points[m] = dot(vol_basis, state_low[m])

    elem_ids = lax.broadcasted_iota(jnp.int32, (elems, elems), 0).astype(F32).astype(BF16)
    one_low = jnp.ones((elems, elems), BF16)
    zero_low = jnp.zeros((elems, elems), BF16)
    for f in range(4):
        source = target[f : f + 1]
        near = kind[f : f + 1] == 0
        for g in range(4):
            hit = near & (source >= g * elems) & (source < (g + 1) * elems)
            wanted = jnp.where(hit, source - g * elems, -1).astype(F32).astype(BF16)
            pick[g * elems : (g + 1) * elems, :] = jnp.where(elem_ids == wanted, one_low, zero_low)
        gathered[:, f * elems : (f + 1) * elems] = dot(turned[...], pick[...])

    loads["normals"].wait()
    loads["areas"].wait()
    spread = one_hot(
        (4 * QP, 4 * face_q), lambda r, c: (c == (r % QP) * 4 + r // QP) & (r % QP < face_q)
    )
    for i in range(3):
        flat = normals[i].astype(F32).reshape(4 * face_q, elems).astype(BF16)
        normal_rows[i] = dot(spread, flat)
    flat = areas[...].reshape(4 * face_q, elems)
    high = flat.astype(BF16)
    low = (flat - high.astype(F32)).astype(BF16)
    area_rows[...] = dot(spread, high) + dot(spread, low)

    loads["vol_grad"].wait()
    loads["face_lift"].wait()

    def sent_point(h):
        def hit(k, c):
            step = h * (span // unit) + c // unit
            sender = step
            if direct:
                sender = partner(row, step, rows)
            return k == sender * unit + c % unit

        return hit

    for h in range(2):
        order = one_hot((vol_q, span), sent_point(h))
        for d in range(3):
            at = h * tile + d * span
            tests[:, at : at + span] = dot(vol_grad[d], order).astype(BF16)
    flat = face_lift[...].reshape(4 * face_q, basis).astype(BF16)
    for h in range(2):
        place = one_hot(
            (4 * face_q, 2 * QP),
            lambda r, c: (r == (c % QP) * 4 + 2 * h + c // QP) & (c % QP < face_q),
        )
        tests[:, h * tile + 3 * span : (h + 1) * tile] = (-dot(flat, place, 0, 0)).astype(BF16)

    lame = material[0:1, :]
    rigid = material[1:2, :]
    light = material[2:3, :]

    def volume_part(step, start, count, read):
        h = step // (span // unit)
        base = h * tile + (step - h * (span // unit)) * unit
        for half in range(elems // 128):
            cut = slice(half * 128, (half + 1) * 128)
            values = [points[m, pl.ds(start, count), cut] for m in range(9)]
            press = [-lame[:, cut] * values[6 + i] for i in range(3)]
            shear = [-rigid[:, cut] * values[6 + i] for i in range(3)]
            force = [-light[:, cut] * values[i] for i in range(6)]
            for d in range(3):
                n = [read(3 * d + i, cut) for i in range(3)]
                results = normal_flux(press, shear, force, n)
                at = base + d * span
                for m in range(9):
                    fluxes[m, at : at + count, cut] = results[m].astype(BF16)

    def volume_half(h):
        count = span // unit
        if direct:
            for step in range(h * count, (h + 1) * count):
                geo_copies[step].wait()
                sender = partner(row, step, rows)
                volume_part(
                    step,
                    pl.multiple_of(sender * local_q, local_q),
                    local_q,
                    lambda k, cut: metric[step, k, :, cut].astype(F32),
                )
        else:
            if h == 0:
                for step in range(rows):
                    geo_copies[step].wait()
                    metric_by_row[partner(row, step, rows)] = metric[step].astype(F32)
            group = 16 // local_q
            for block in range(h * count, (h + 1) * count):
                volume_part(
                    block,
                    block * 16,
                    16,
                    lambda k, cut: jnp.concatenate(
                        [metric_by_row[block * group + j, k, :, cut] for j in range(group)], axis=0
                    ),
                )

    pool_ids = lax.broadcasted_iota(jnp.int32, (cols * slots, elems), 0)
    for f in range(4):
        wanted = jnp.where(
            kind[f : f + 1] == 1, peer_index[f : f + 1] * slots + target[f : f + 1], -1
        )
        far[:, f * elems : (f + 1) * elems] = jnp.where(pool_ids == wanted, 1.0, 0.0).astype(BF16)
    own_speed = jnp.sqrt((lame + 2.0 * rigid) * light)

    def surface_face(f):
        lanes = slice(f * elems, (f + 1) * elems)
        free = jnp.where(kind[f : f + 1] == 2, 1.0, 0.0)
        edge = jnp.where(kind[f : f + 1] >= 2, 1.0, 0.0)
        other = []
        for i in range(3):
            high_at = i * QP + face_q
            low_at = (i + 3) * QP + face_q
            other.append(
                gathered[high_at : high_at + 1, lanes]
                + gathered[low_at : low_at + 1, lanes]
                + edge * material[i : i + 1, :]
            )
        speed = jnp.sqrt((other[0] + 2.0 * other[1]) * other[2])
        penalty_scale = 0.5 * jnp.maximum(own_speed, speed)
        for half in range(elems // 128):
            cut = slice(half * 128, (half + 1) * 128)
            a0, a1, a2 = -0.5 * lame[:, cut], -0.5 * rigid[:, cut], -0.5 * light[:, cut]
            b0, b1, b2 = -0.5 * other[0][:, cut], -0.5 * other[1][:, cut], -0.5 * other[2][:, cut]
            mirror = free[:, cut]
            for part in range(QP // 16):
                at = f * QP + part * 16
                n = [normal_rows[i, at : at + 16, cut] for i in range(3)]
                pen = penalty_scale[:, cut] * area_rows[at : at + 16, cut]
                own = [traces[m, at : at + 16, cut] for m in range(9)]
                met = []
                for m in range(9):
                    top = m * QP + part * 16
                    left = f * elems + half * 128
                    value = gathered[top : top + 16, left : left + 128]
                    part_own = mirror * own[m]
                    met.append(value - part_own if m < 6 else value + part_own)
                press = [a0 * own[6 + i] + b0 * met[6 + i] for i in range(3)]
                shear = [a1 * own[6 + i] + b1 * met[6 + i] for i in range(3)]
                force = [a2 * own[i] + b2 * met[i] for i in range(6)]
                results = normal_flux(press, shear, force, n)
                to = (f // 2) * tile + 3 * span + (f % 2) * QP + part * 16
                for m in range(9):
                    total = results[m] + pen * (own[m] - met[m])
                    fluxes[m, to : to + 16, cut] = total.astype(BF16)

    factor = material[3:4, :]
    volume_half(0)
    for copy in face_copies:
        copy.wait()
    received = pool[...].reshape(cols * slots, quantities * QP)
    gathered[...] = gathered[...] + dot(received, far[...], 0, 0)
    surface_face(0)
    surface_face(1)
    for m in range(quantities):
        out[m] = state[m] + factor * dot(tests[:, 0:tile], fluxes[m, 0:tile, :])
    surface_face(2)
    surface_face(3)
    volume_half(1)
    for m in range(quantities):
        out[m] = out[m] + factor * dot(tests[:, tile : 2 * tile], fluxes[m, tile : 2 * tile, :])


def normal_flux(press, shear, force, n):
    pressure = press[0] * n[0] + press[1] * n[1] + press[2] * n[2]
    twice = [shear[i] + shear[i] for i in range(3)]
    return [
        pressure + twice[0] * n[0],
        pressure + twice[1] * n[1],
        pressure + twice[2] * n[2],
        n[0] * shear[1] + n[1] * shear[0],
        n[1] * shear[2] + n[2] * shear[1],
        n[0] * shear[2] + n[2] * shear[0],
        force[0] * n[0] + force[3] * n[1] + force[5] * n[2],
        force[3] * n[0] + force[1] * n[1] + force[4] * n[2],
        force[5] * n[0] + force[4] * n[1] + force[2] * n[2],
    ]


def per_device(
    rows,
    cols,
    state,
    geometry,
    material,
    neighbours,
    send_faces,
    vol_eval,
    vol_grad,
    face_eval,
    face_lift,
    normals,
    areas,
):
    quantities, basis, elems = state.shape
    slots = send_faces.shape[2]
    vol_q = vol_eval.shape[1]
    local_q = geometry.shape[1]
    total = 3 * vol_q + 4 * QP
    operands = [
        state,
        geometry,
        material,
        neighbours,
        send_faces,
        vol_eval,
        vol_grad,
        jnp.transpose(face_eval, (2, 0, 1)),
        jnp.transpose(face_lift, (2, 0, 1)),
        normals,
        areas,
    ]
    staged = [pltpu.VMEM(x.shape, x.dtype) for x in operands[:1] + operands[2:]]
    scratch = staged + [
        pltpu.VMEM((rows, 9, local_q, elems), BF16),
        pltpu.VMEM((quantities, basis, elems), BF16),
        pltpu.VMEM((quantities, 4 * QP, elems), F32),
        pltpu.VMEM((quantities * QP, 4 * elems), BF16),
        pltpu.VMEM((cols, slots, quantities * QP), BF16),
        pltpu.VMEM((cols, slots, quantities * QP), BF16),
        pltpu.VMEM((quantities * QP, 4 * elems), F32),
        pltpu.VMEM((quantities, vol_q, elems), F32),
        pltpu.VMEM((quantities, total, elems), BF16),
        pltpu.VMEM((basis, total), BF16),
        pltpu.VMEM((3, 4 * QP, elems), F32),
        pltpu.VMEM((4 * QP, elems), F32),
        pltpu.VMEM((4 * elems, elems), BF16),
        pltpu.VMEM((cols * slots, 4 * elems), BF16),
        pltpu.SemaphoreType.DMA((len(staged),)),
        pltpu.SemaphoreType.DMA((rows,)),
        pltpu.SemaphoreType.DMA((rows,)),
        pltpu.SemaphoreType.DMA((cols,)),
        pltpu.SemaphoreType.DMA((cols,)),
    ]
    if local_q % 16 != 0:
        scratch.append(pltpu.VMEM((rows, 9, local_q, elems), F32))
    return pl.pallas_call(
        functools.partial(kernel, rows, cols),
        out_shape=jax.ShapeDtypeStruct(state.shape, F32),
        in_specs=[pl.BlockSpec(memory_space=pltpu.HBM)] * len(operands),
        out_specs=pl.BlockSpec(memory_space=pltpu.VMEM),
        scratch_shapes=scratch,
        compiler_params=pltpu.CompilerParams(
            collective_id=0, has_side_effects=True, vmem_limit_bytes=48 * 1024 * 1024
        ),
    )(*[pltpu.with_memory_space_constraint(x, pltpu.HBM) for x in operands])


def solution(mesh):
    return jax.shard_map(
        functools.partial(per_device, mesh.shape["row"], mesh.shape["col"]),
        mesh=mesh,
        in_specs=(
            P(None, None, ("col", "row")),
            P(None, "row", "col"),
            P(None, ("col", "row")),
            P(None, None, ("col", "row")),
            P(("col", "row"), None, None),
            P(),
            P(),
            P(),
            P(),
            P(None, None, None, ("col", "row")),
            P(None, None, ("col", "row")),
        ),
        out_specs=P(None, None, ("col", "row")),
        check_vma=False,
    )
```

profile of v0, /device:TPU:0, one launch (start us, length us, event | category | flops | bytes accessed | tf_op | source)
XLA Modules:
  0.0 15.5 jit_solution(14837814554928298440)
XLA Ops:
  0.0 14.8 %shard_map.109 = f32[9,35,256]{2,1,0:T(8,128)S(1)} custom-call(f32[9,35,256]{2,1,0:T(8,128)} %state_in.1, bf16[9,16,2048]{2,1,0:T(8,128)(2,1)} %geometry.1, f32[4,256]{1,0:T(4,128)} %material_in.1, s32[4,4,256]{2,1,0:T(4,128)} %neighbours_in.1, s32[1,4,64]{2,1,0:T(4,128)} %send_in.1, f32[35,128]{1,0:T(8,128)} %vol_eval_in.1, ...), custom_call_target="tpu_custom_call" | custom-call | tf_op jit(solution)/shard_map/pallas_call | solution.py:467
  14.8 0.7 %copy.13 = f32[9,35,256]{2,1,0:T(8,128)} copy(f32[9,35,256]{2,1,0:T(8,128)S(1)} %shard_map.109) | data formatting | bytes 645120
where the time goes:
time: 15.7 us; the launch traced here: 15.5 us
  Pallas kernels  14.8 us (94%)
  local copies, waits for them, and re-layouts  0.74 us (5%)
    pallas_call x1, Pallas kernels, per_device(): pl.pallas_call(functools.partial(kernel, rows, cols), out_shape=jax.Shape...  14.8 us
    unnamed x1, local copies, waits for them, and re-layouts  0.74 us

commit v1 on v0

--- a/solution.py
+++ b/solution.py
@@ -28,6 +28,31 @@
         total = total + ((row // bit + step // bit) % 2) * bit
         bit *= 2
     return total
+
+
+class Order:
+    def __init__(self, row, rows):
+        self.row, self.rows = row, rows
+
+    def shared(self, step):
+        bits = [b for b in range(1, self.rows.bit_length()) if (step >> b) & 1]
+        return sum((self.row // (1 << b)) % 2 for b in bits), len(bits)
+
+    def earlier(self, step):
+        if step == 1:
+            return self.row % 2 == 0
+        held, count = self.shared(step)
+        return held == count
+
+    def later(self, step):
+        if step == 1:
+            return self.row % 2 == 1
+        held, _ = self.shared(step)
+        return held == 0
+
+    def apart(self, step):
+        held, count = self.shared(step)
+        return (held > 0) & (held < count)
 
 
 def one_hot(shape, hit):
@@ -80,6 +105,8 @@
     geo_recv,
     face_send,
     face_recv,
+    row_in,
+    col_in,
     metric_by_row=None,
 ):
     row = lax.axis_index("row")
@@ -96,14 +123,34 @@
     paired = rows & (rows - 1) == 0
 
     barrier = pltpu.get_barrier_semaphore()
-    for step in range(1, rows):
-        pl.semaphore_signal(
-            barrier, inc=1, device_id={"row": lax.rem(row + step, rows)}, device_id_type=MESH
-        )
-    for step in range(1, cols):
-        pl.semaphore_signal(
-            barrier, inc=1, device_id={"col": lax.rem(col + step, cols)}, device_id_type=MESH
-        )
+    ordered = paired and rows > 1
+    if ordered:
+        order = Order(row, rows)
+        for step in range(1, rows):
+
+            @pl.when(order.later(step))
+            def _():
+                pl.semaphore_signal(
+                    barrier,
+                    inc=1,
+                    device_id={"row": partner(row, step, rows)},
+                    device_id_type=MESH,
+                )
+
+        for other in range(1, cols):
+
+            @pl.when(col < other)
+            def _():
+                pl.semaphore_signal(barrier, inc=1, device_id={"col": other}, device_id_type=MESH)
+    else:
+        for step in range(1, rows):
+            pl.semaphore_signal(
+                barrier, inc=1, device_id={"row": lax.rem(row + step, rows)}, device_id_type=MESH
+            )
+        for step in range(1, cols):
+            pl.semaphore_signal(
+                barrier, inc=1, device_id={"col": lax.rem(col + step, cols)}, device_id_type=MESH
+            )
     loads = {}
     pairs = [
         ("state", state_in, state),
@@ -126,12 +173,9 @@
         geo_recv.at[0],
     )
     own_copy.start()
-    pl.semaphore_wait(barrier, rows + cols - 2)
-
-    geo_copies = [own_copy]
-    for step in range(1, rows):
+    def geo_copy(step):
         peer = partner(row, step, rows) if paired else lax.rem(row + step, rows)
-        copy = pltpu.make_async_remote_copy(
+        return pltpu.make_async_remote_copy(
             src_ref=geometry.at[:, :, pl.ds(pl.multiple_of(peer * elems, 128), elems)],
             dst_ref=metric.at[step],
             send_sem=geo_send.at[step],
@@ -139,8 +183,55 @@
             device_id={"row": peer},
             device_id_type=MESH,
         )
-        copy.start()
-        geo_copies.append(copy)
+
+    def face_copy(step):
+        peer = lax.rem(col + step, cols)
+        return pltpu.make_async_remote_copy(
+            src_ref=outgoing.at[peer],
+            dst_ref=pool.at[col],
+            send_sem=face_send.at[step],
+            recv_sem=face_recv.at[step],
+            device_id={"col": peer},
+            device_id_type=MESH,
+        )
+
+    geo_copies = [own_copy] + [geo_copy(step) for step in range(1, rows)]
+    if ordered:
+        due = col + sum(jnp.where(order.earlier(step), 1, 0) for step in range(1, rows))
+
+        @pl.when(due > 0)
+        def _():
+            pl.semaphore_wait(barrier, due)
+
+        for step in range(1, rows):
+
+            @pl.when(order.earlier(step))
+            def _():
+                pl.semaphore_signal(
+                    row_in.at[step],
+                    inc=1,
+                    device_id={"row": partner(row, step, rows)},
+                    device_id_type=MESH,
+                )
+
+        for step in range(1, rows):
+
+            @pl.when(order.earlier(step))
+            def _():
+                geo_copies[step].start()
+
+        for step in range(1, cols):
+
+            @pl.when(col >= step)
+            def _():
+                pl.semaphore_signal(
+                    col_in.at[step], inc=1, device_id={"col": col - step}, device_id_type=MESH
+                )
+
+    else:
+        pl.semaphore_wait(barrier, rows + cols - 2)
+        for step in range(1, rows):
+            geo_copies[step].start()
 
     pool[col] = jnp.zeros((slots, quantities * QP), BF16)
     loads["face_eval"].wait()
@@ -206,25 +297,43 @@
     for p in range(cols):
         outgoing[p] = listed_traces[p * slots : (p + 1) * slots]
 
-    face_copies = []
+    if ordered:
+        for step in range(1, rows):
+
+            @pl.when(order.later(step))
+            def _():
+                pl.semaphore_wait(row_in.at[step], 1)
+                geo_copies[step].start()
+
+        for step in range(1, rows):
+            if (step // 2) & (step // 2 - 1):
+
+                @pl.when(order.apart(step))
+                def _():
+                    geo_copies[step].start()
+    face_copies = [face_copy(step) for step in range(1, cols)]
     for step in range(1, cols):
-        peer = lax.rem(col + step, cols)
-        copy = pltpu.make_async_remote_copy(
-            src_ref=outgoing.at[peer],
-            dst_ref=pool.at[col],
-            send_sem=face_send.at[step],
-            recv_sem=face_recv.at[step],
-            device_id={"col": peer},
-            device_id_type=MESH,
-        )
-        copy.start()
-        face_copies.append(copy)
+        if ordered:
+
+            @pl.when(col + step >= cols)
+            def _():
+                face_copies[step - 1].start()
+        else:
+            face_copies[step - 1].start()
 
     loads["vol_eval"].wait()
     same_q = one_hot((vol_q, vol_q), lambda r, c: r == c)
     vol_basis = dot(same_q, vol_eval[...].astype(BF16), 1, 1).astype(BF16)
     for m in range(quantities):
         points[m] = dot(vol_basis, state_low[m])
+
+    if ordered:
+        for step in range(1, cols):
+
+            @pl.when(col + step < cols)
+            def _():
+                pl.semaphore_wait(col_in.at[step], 1)
+                face_copies[step - 1].start()
 
     elem_ids = lax.broadcasted_iota(jnp.int32, (elems, elems), 0).astype(F32).astype(BF16)
     one_low = jnp.ones((elems, elems), BF16)
@@ -461,6 +570,8 @@
         pltpu.SemaphoreType.DMA((rows,)),
         pltpu.SemaphoreType.DMA((cols,)),
         pltpu.SemaphoreType.DMA((cols,)),
+        pltpu.SemaphoreType.REGULAR((rows,)),
+        pltpu.SemaphoreType.REGULAR((cols,)),
     ]
     if local_q % 16 != 0:
         scratch.append(pltpu.VMEM((rows, 9, local_q, elems), F32))

time: 15.7 us -> 14.7 us (0.936)
  Pallas kernels: 14.8 us -> 13.8 us
    pallas_call x1, Pallas kernels: 14.8 us -> 13.8 us  [per_device(): pl.pallas_call(functools.partial(kernel, rows, cols), out_shape=jax.Shape...]
where the time goes in v1:
time: 14.7 us; the launch traced here: 14.5 us
  Pallas kernels  13.8 us (94%)
  local copies, waits for them, and re-layouts  0.74 us (5%)
    pallas_call x1, Pallas kernels, per_device(): pl.pallas_call(functools.partial(kernel, rows, cols), out_shape=jax.Shape...  13.8 us
    unnamed x1, local copies, waits for them, and re-layouts  0.74 us

profile of v1, /device:TPU:0, one launch (start us, length us, event | category | flops | bytes accessed | tf_op | source)
XLA Modules:
  0.0 14.5 jit_solution(730804977515591937)
XLA Ops:
  0.0 13.8 %shard_map.109 = f32[9,35,256]{2,1,0:T(8,128)S(1)} custom-call(f32[9,35,256]{2,1,0:T(8,128)} %state_in.1, bf16[9,16,2048]{2,1,0:T(8,128)(2,1)} %geometry.1, f32[4,256]{1,0:T(4,128)} %material_in.1, s32[4,4,256]{2,1,0:T(4,128)} %neighbours_in.1, s32[1,4,64]{2,1,0:T(4,128)} %send_in.1, f32[35,128]{1,0:T(8,128)} %vol_eval_in.1, ...), custom_call_target="tpu_custom_call" | custom-call | tf_op jit(solution)/shard_map/pallas_call | solution.py:578
  13.8 0.7 %copy.13 = f32[9,35,256]{2,1,0:T(8,128)} copy(f32[9,35,256]{2,1,0:T(8,128)S(1)} %shard_map.109) | data formatting | bytes 645120

commit v2 on v1

--- a/solution.py
+++ b/solution.py
@@ -53,6 +53,18 @@
     def apart(self, step):
         held, count = self.shared(step)
         return (held > 0) & (held < count)
+
+
+def tiles(vol_q, unit):
+    count = vol_q // unit
+    groups = [list(range(count - 3)), [count - 3], [count - 2, count - 1]]
+    depths = [3 * unit * len(steps) for steps in groups]
+    depths[1] += 4 * QP
+    flux_at = [0, depths[0], depths[0] + depths[1]]
+    tests_at = [0]
+    for depth in depths:
+        tests_at.append(tests_at[-1] + (depth + 127) // 128 * 128)
+    return groups, depths, flux_at, tests_at
 
 
 def one_hot(shape, hit):
@@ -117,9 +129,8 @@
     face_q = face_eval.shape[0]
     slots = send_faces.shape[2]
     direct = local_q % 16 == 0
-    unit = local_q if direct else 16
-    span = vol_q // 2
-    tile = 3 * span + 2 * QP
+    unit = max(local_q, 16)
+    groups, depths, flux_at, tests_at = tiles(vol_q, unit)
     paired = rows & (rows - 1) == 0
 
     barrier = pltpu.get_barrier_semaphore()
@@ -152,21 +163,28 @@
                 barrier, inc=1, device_id={"col": lax.rem(col + step, cols)}, device_id_type=MESH
             )
     loads = {}
-    pairs = [
-        ("state", state_in, state),
-        ("face_eval", face_eval_in, face_eval),
-        ("material", material_in, material),
-        ("neighbours", neighbours_in, neighbours),
-        ("send_faces", send_in, send_faces),
-        ("vol_eval", vol_eval_in, vol_eval),
-        ("normals", normals_in, normals),
-        ("areas", areas_in, areas),
-        ("vol_grad", vol_grad_in, vol_grad),
-        ("face_lift", face_lift_in, face_lift),
+    groups_of_loads = [
+        [
+            (face_eval_in, face_eval),
+            (state_in, state),
+            (material_in, material),
+            (neighbours_in, neighbours),
+            (send_in, send_faces),
+        ],
+        [
+            (vol_eval_in, vol_eval),
+            (normals_in, normals),
+            (areas_in, areas),
+            (vol_grad_in, vol_grad),
+            (face_lift_in, face_lift),
+        ],
     ]
-    for index, (name, source, target) in enumerate(pairs):
-        loads[name] = pltpu.make_async_copy(source, target, load_sem.at[index])
-        loads[name].start()
+    for index, group in enumerate(groups_of_loads):
+        loads[index] = [
+            pltpu.make_async_copy(source, target, load_sem.at[index]) for source, target in group
+        ]
+        for copy in loads[index]:
+            copy.start()
     own_copy = pltpu.make_async_copy(
         geometry.at[:, :, pl.ds(pl.multiple_of(row * elems, 128), elems)],
         metric.at[0],
@@ -178,7 +196,7 @@
         return pltpu.make_async_remote_copy(
             src_ref=geometry.at[:, :, pl.ds(pl.multiple_of(peer * elems, 128), elems)],
             dst_ref=metric.at[step],
-            send_sem=geo_send.at[step],
+            send_sem=geo_send,
             recv_sem=geo_recv.at[step],
             device_id={"row": peer},
             device_id_type=MESH,
@@ -189,8 +207,8 @@
         return pltpu.make_async_remote_copy(
             src_ref=outgoing.at[peer],
             dst_ref=pool.at[col],
-            send_sem=face_send.at[step],
-            recv_sem=face_recv.at[step],
+            send_sem=face_send,
+            recv_sem=face_recv,
             device_id={"col": peer},
             device_id_type=MESH,
         )
@@ -208,7 +226,7 @@
             @pl.when(order.earlier(step))
             def _():
                 pl.semaphore_signal(
-                    row_in.at[step],
+                    row_in.at[step - 1],
                     inc=1,
                     device_id={"row": partner(row, step, rows)},
                     device_id_type=MESH,
@@ -225,7 +243,7 @@
             @pl.when(col >= step)
             def _():
                 pl.semaphore_signal(
-                    col_in.at[step], inc=1, device_id={"col": col - step}, device_id_type=MESH
+                    col_in.at[step - 1], inc=1, device_id={"col": col - step}, device_id_type=MESH
                 )
 
     else:
@@ -234,7 +252,6 @@
             geo_copies[step].start()
 
     pool[col] = jnp.zeros((slots, quantities * QP), BF16)
-    loads["face_eval"].wait()
 
     def turning_rows(r, c):
         f = r // (3 * QP)
@@ -246,13 +263,13 @@
         return (c == (q - k + moved) * 4 + f) & (q < face_q)
 
     turning = one_hot((12 * QP, 4 * face_q), turning_rows)
+    same = one_hot((slots, slots), lambda r, c: r == c)
+    for copy in loads[0]:
+        copy.wait()
     flat = face_eval[...].reshape(4 * face_q, basis).astype(BF16)
     face_basis = dot(turning, flat).astype(BF16)
-    loads["state"].wait()
     for m in range(quantities):
         state_low[m] = state[m].astype(BF16)
-    loads["material"].wait()
-    loads["neighbours"].wait()
     kind = neighbours[0]
     peer_index = neighbours[1]
     target = neighbours[2]
@@ -277,8 +294,6 @@
                 chosen = jnp.where(row_ids == face_q, low_rows[m], chosen)
             turned[m * QP : (m + 1) * QP, f * elems : (f + 1) * elems] = chosen.astype(BF16)
 
-    loads["send_faces"].wait()
-    same = one_hot((slots, slots), lambda r, c: r == c)
     listed = send_faces[0]
     listed_face = listed // elems
     listed_elem = listed - listed_face * elems
@@ -297,12 +312,22 @@
     for p in range(cols):
         outgoing[p] = listed_traces[p * slots : (p + 1) * slots]
 
+    face_copies = [face_copy(step) for step in range(1, cols)]
+    for step in range(1, cols):
+        if ordered:
+
+            @pl.when(col + step >= cols)
+            def _():
+                face_copies[step - 1].start()
+        else:
+            face_copies[step - 1].start()
+
     if ordered:
         for step in range(1, rows):
 
             @pl.when(order.later(step))
             def _():
-                pl.semaphore_wait(row_in.at[step], 1)
+                pl.semaphore_wait(row_in.at[step - 1], 1)
                 geo_copies[step].start()
 
         for step in range(1, rows):
@@ -311,17 +336,9 @@
                 @pl.when(order.apart(step))
                 def _():
                     geo_copies[step].start()
-    face_copies = [face_copy(step) for step in range(1, cols)]
-    for step in range(1, cols):
-        if ordered:
-
-            @pl.when(col + step >= cols)
-            def _():
-                face_copies[step - 1].start()
-        else:
-            face_copies[step - 1].start()
-
-    loads["vol_eval"].wait()
+
+    for copy in loads[1]:
+        copy.wait()
     same_q = one_hot((vol_q, vol_q), lambda r, c: r == c)
     vol_basis = dot(same_q, vol_eval[...].astype(BF16), 1, 1).astype(BF16)
     for m in range(quantities):
@@ -332,7 +349,7 @@
 
             @pl.when(col + step < cols)
             def _():
-                pl.semaphore_wait(col_in.at[step], 1)
+                pl.semaphore_wait(col_in.at[step - 1], 1)
                 face_copies[step - 1].start()
 
     elem_ids = lax.broadcasted_iota(jnp.int32, (elems, elems), 0).astype(F32).astype(BF16)
@@ -347,8 +364,6 @@
             pick[g * elems : (g + 1) * elems, :] = jnp.where(elem_ids == wanted, one_low, zero_low)
         gathered[:, f * elems : (f + 1) * elems] = dot(turned[...], pick[...])
 
-    loads["normals"].wait()
-    loads["areas"].wait()
     spread = one_hot(
         (4 * QP, 4 * face_q), lambda r, c: (c == (r % QP) * 4 + r // QP) & (r % QP < face_q)
     )
@@ -360,39 +375,35 @@
     low = (flat - high.astype(F32)).astype(BF16)
     area_rows[...] = dot(spread, high) + dot(spread, low)
 
-    loads["vol_grad"].wait()
-    loads["face_lift"].wait()
-
-    def sent_point(h):
-        def hit(k, c):
-            step = h * (span // unit) + c // unit
-            sender = step
-            if direct:
-                sender = partner(row, step, rows)
+
+    for t, steps in enumerate(groups):
+        wide = len(steps) * unit
+
+        def sent_point(k, c):
+            step = steps[0] + c // unit
+            sender = partner(row, step, rows) if direct else step
             return k == sender * unit + c % unit
 
-        return hit
-
-    for h in range(2):
-        order = one_hot((vol_q, span), sent_point(h))
+        chosen_q = one_hot((vol_q, wide), sent_point)
         for d in range(3):
-            at = h * tile + d * span
-            tests[:, at : at + span] = dot(vol_grad[d], order).astype(BF16)
+            at = tests_at[t] + d * wide
+            tests[:, at : at + wide] = dot(vol_grad[d], chosen_q).astype(BF16)
     flat = face_lift[...].reshape(4 * face_q, basis).astype(BF16)
-    for h in range(2):
-        place = one_hot(
-            (4 * face_q, 2 * QP),
-            lambda r, c: (r == (c % QP) * 4 + 2 * h + c // QP) & (c % QP < face_q),
-        )
-        tests[:, h * tile + 3 * span : (h + 1) * tile] = (-dot(flat, place, 0, 0)).astype(BF16)
+    place = one_hot(
+        (4 * face_q, 4 * QP),
+        lambda r, c: (r == (c % QP) * 4 + c // QP) & (c % QP < face_q),
+    )
+    at = tests_at[1] + 3 * unit * len(groups[1])
+    tests[:, at : at + 4 * QP] = (-dot(flat, place, 0, 0)).astype(BF16)
 
     lame = material[0:1, :]
     rigid = material[1:2, :]
     light = material[2:3, :]
 
     def volume_part(step, start, count, read):
-        h = step // (span // unit)
-        base = h * tile + (step - h * (span // unit)) * unit
+        t = [step in steps for steps in groups].index(True)
+        wide = len(groups[t]) * unit
+        base = flux_at[t] + (step - groups[t][0]) * unit
         for half in range(elems // 128):
             cut = slice(half * 128, (half + 1) * 128)
             values = [points[m, pl.ds(start, count), cut] for m in range(9)]
@@ -402,15 +413,20 @@
             for d in range(3):
                 n = [read(3 * d + i, cut) for i in range(3)]
                 results = normal_flux(press, shear, force, n)
-                at = base + d * span
+                at = base + d * wide
                 for m in range(9):
                     fluxes[m, at : at + count, cut] = results[m].astype(BF16)
 
-    def volume_half(h):
-        count = span // unit
+    def arrived(step):
+        if step == 0:
+            own_copy.wait()
+        else:
+            geo_copies[step].wait_recv()
+
+    def volume(steps):
         if direct:
-            for step in range(h * count, (h + 1) * count):
-                geo_copies[step].wait()
+            for step in steps:
+                arrived(step)
                 sender = partner(row, step, rows)
                 volume_part(
                     step,
@@ -419,12 +435,12 @@
                     lambda k, cut: metric[step, k, :, cut].astype(F32),
                 )
         else:
-            if h == 0:
+            if steps[0] == 0:
                 for step in range(rows):
-                    geo_copies[step].wait()
+                    arrived(step)
                     metric_by_row[partner(row, step, rows)] = metric[step].astype(F32)
             group = 16 // local_q
-            for block in range(h * count, (h + 1) * count):
+            for block in steps:
                 volume_part(
                     block,
                     block * 16,
@@ -433,6 +449,10 @@
                         [metric_by_row[block * group + j, k, :, cut] for j in range(group)], axis=0
                     ),
                 )
+
+    def contract(t, m):
+        left = tests[:, tests_at[t] : tests_at[t] + depths[t]]
+        return dot(left, fluxes[m, flux_at[t] : flux_at[t] + depths[t], :])
 
     pool_ids = lax.broadcasted_iota(jnp.int32, (cols * slots, elems), 0)
     for f in range(4):
@@ -478,26 +498,31 @@
                 shear = [a1 * own[6 + i] + b1 * met[6 + i] for i in range(3)]
                 force = [a2 * own[i] + b2 * met[i] for i in range(6)]
                 results = normal_flux(press, shear, force, n)
-                to = (f // 2) * tile + 3 * span + (f % 2) * QP + part * 16
+                to = flux_at[1] + 3 * unit * len(groups[1]) + f * QP + part * 16
                 for m in range(9):
                     total = results[m] + pen * (own[m] - met[m])
                     fluxes[m, to : to + 16, cut] = total.astype(BF16)
 
     factor = material[3:4, :]
-    volume_half(0)
-    for copy in face_copies:
-        copy.wait()
+    volume(groups[0])
+    for m in range(quantities):
+        out[m] = contract(0, m)
+    volume(groups[1])
+    whole = pool.at[pl.ds(0, cols - 1)]
+    pltpu.make_async_copy(whole, whole, face_recv).wait()
     received = pool[...].reshape(cols * slots, quantities * QP)
     gathered[...] = gathered[...] + dot(received, far[...], 0, 0)
-    surface_face(0)
-    surface_face(1)
+    for f in range(4):
+        surface_face(f)
     for m in range(quantities):
-        out[m] = state[m] + factor * dot(tests[:, 0:tile], fluxes[m, 0:tile, :])
-    surface_face(2)
-    surface_face(3)
-    volume_half(1)
+        out[m] = out[m] + contract(1, m)
+    volume(groups[2])
+    whole = metric.at[pl.ds(0, rows - 1)]
+    pltpu.make_async_copy(whole, whole, geo_send).wait()
+    whole = outgoing.at[pl.ds(0, cols - 1)]
+    pltpu.make_async_copy(whole, whole, face_send).wait()
     for m in range(quantities):
-        out[m] = out[m] + factor * dot(tests[:, tile : 2 * tile], fluxes[m, tile : 2 * tile, :])
+        out[m] = state[m] + factor * (out[m] + contract(2, m))
 
 
 def normal_flux(press, shear, force, n):
@@ -536,6 +561,7 @@
     vol_q = vol_eval.shape[1]
     local_q = geometry.shape[1]
     total = 3 * vol_q + 4 * QP
+    tests_at = tiles(vol_q, max(local_q, 16))[3]
     operands = [
         state,
         geometry,
@@ -560,18 +586,18 @@
         pltpu.VMEM((quantities * QP, 4 * elems), F32),
         pltpu.VMEM((quantities, vol_q, elems), F32),
         pltpu.VMEM((quantities, total, elems), BF16),
-        pltpu.VMEM((basis, total), BF16),
+        pltpu.VMEM((basis, tests_at[-1]), BF16),
         pltpu.VMEM((3, 4 * QP, elems), F32),
         pltpu.VMEM((4 * QP, elems), F32),
         pltpu.VMEM((4 * elems, elems), BF16),
         pltpu.VMEM((cols * slots, 4 * elems), BF16),
-        pltpu.SemaphoreType.DMA((len(staged),)),
+        pltpu.SemaphoreType.DMA((2,)),
+        pltpu.SemaphoreType.DMA,
         pltpu.SemaphoreType.DMA((rows,)),
-        pltpu.SemaphoreType.DMA((rows,)),
-        pltpu.SemaphoreType.DMA((cols,)),
-        pltpu.SemaphoreType.DMA((cols,)),
-        pltpu.SemaphoreType.REGULAR((rows,)),
-        pltpu.SemaphoreType.REGULAR((cols,)),
+        pltpu.SemaphoreType.DMA,
+        pltpu.SemaphoreType.DMA,
+        pltpu.SemaphoreType.REGULAR((rows - 1,)),
+        pltpu.SemaphoreType.REGULAR((cols - 1,)),
     ]
     if local_q % 16 != 0:
         scratch.append(pltpu.VMEM((rows, 9, local_q, elems), F32))

time: 14.7 us -> 12.9 us (0.88)
  Pallas kernels: 13.8 us -> 12 us
    pallas_call x1, Pallas kernels: 13.8 us -> 12 us  [per_device(): pl.pallas_call(functools.partial(kernel, rows, cols), out_shape=jax.Shape...]
where the time goes in v2:
time: 12.9 us; the launch traced here: 12.8 us
  Pallas kernels  12 us (93%)
  local copies, waits for them, and re-layouts  0.74 us (6%)
    pallas_call x1, Pallas kernels, per_device(): pl.pallas_call(functools.partial(kernel, rows, cols), out_shape=jax.Shape...  12 us
    unnamed x1, local copies, waits for them, and re-layouts  0.74 us

profile of v2, /device:TPU:0, one launch (start us, length us, event | category | flops | bytes accessed | tf_op | source)
XLA Modules:
  0.0 12.8 jit_solution(11041355714223025603)
XLA Ops:
  0.0 12.0 %shard_map.109 = f32[9,35,256]{2,1,0:T(8,128)S(1)} custom-call(f32[9,35,256]{2,1,0:T(8,128)} %state_in.1, bf16[9,16,2048]{2,1,0:T(8,128)(2,1)} %geometry.1, f32[4,256]{1,0:T(4,128)} %material_in.1, s32[4,4,256]{2,1,0:T(4,128)} %neighbours_in.1, s32[1,4,64]{2,1,0:T(4,128)} %send_in.1, f32[35,128]{1,0:T(8,128)} %vol_eval_in.1, ...), custom_call_target="tpu_custom_call" | custom-call | tf_op jit(solution)/shard_map/pallas_call | solution.py:604
  12.0 0.7 %copy.13 = f32[9,35,256]{2,1,0:T(8,128)} copy(f32[9,35,256]{2,1,0:T(8,128)S(1)} %shard_map.109) | data formatting | bytes 645120

commit v3 on v2

--- a/solution.py
+++ b/solution.py
@@ -57,9 +57,8 @@
 
 def tiles(vol_q, unit):
     count = vol_q // unit
-    groups = [list(range(count - 3)), [count - 3], [count - 2, count - 1]]
-    depths = [3 * unit * len(steps) for steps in groups]
-    depths[1] += 4 * QP
+    groups = [list(range(count - 3)), [count - 3, count - 2, count - 1]]
+    depths = [3 * unit * len(steps) for steps in groups] + [4 * QP]
     flux_at = [0, depths[0], depths[0] + depths[1]]
     tests_at = [0]
     for depth in depths:
@@ -213,6 +212,14 @@
             device_id_type=MESH,
         )
 
+    def later_sends(steps, where=True):
+        for step in steps:
+
+            @pl.when(order.later(step) & where)
+            def _():
+                pl.semaphore_wait(row_in.at[step - 1], 1)
+                geo_copies[step].start()
+
     geo_copies = [own_copy] + [geo_copy(step) for step in range(1, rows)]
     if ordered:
         due = col + sum(jnp.where(order.earlier(step), 1, 0) for step in range(1, rows))
@@ -251,7 +258,8 @@
         for step in range(1, rows):
             geo_copies[step].start()
 
-    pool[col] = jnp.zeros((slots, quantities * QP), BF16)
+    wire = pool.shape[2]
+    pool[col] = jnp.zeros((slots, wire), BF16)
 
     def turning_rows(r, c):
         f = r // (3 * QP)
@@ -264,6 +272,10 @@
 
     turning = one_hot((12 * QP, 4 * face_q), turning_rows)
     same = one_hot((slots, slots), lambda r, c: r == c)
+    narrow = one_hot(
+        (quantities * QP, wire),
+        lambda r, c: (c == (r // QP) * (face_q + 1) + r % QP) & (r % QP <= face_q),
+    )
     for copy in loads[0]:
         copy.wait()
     flat = face_eval[...].reshape(4 * face_q, basis).astype(BF16)
@@ -294,6 +306,16 @@
                 chosen = jnp.where(row_ids == face_q, low_rows[m], chosen)
             turned[m * QP : (m + 1) * QP, f * elems : (f + 1) * elems] = chosen.astype(BF16)
 
+    if ordered:
+        later_sends(range(1, rows - 2))
+        later_sends(range(rows - 2, rows), row >= 2)
+        for step in range(1, rows):
+            if (step // 2) & (step // 2 - 1):
+
+                @pl.when(order.apart(step))
+                def _():
+                    geo_copies[step].start()
+
     listed = send_faces[0]
     listed_face = listed // elems
     listed_elem = listed - listed_face * elems
@@ -309,6 +331,7 @@
         axis=0,
     )
     listed_traces = dot(send_pick, turned[...], 1, 1).astype(BF16)
+    listed_traces = dot(listed_traces, narrow).astype(BF16)
     for p in range(cols):
         outgoing[p] = listed_traces[p * slots : (p + 1) * slots]
 
@@ -323,19 +346,7 @@
             face_copies[step - 1].start()
 
     if ordered:
-        for step in range(1, rows):
-
-            @pl.when(order.later(step))
-            def _():
-                pl.semaphore_wait(row_in.at[step - 1], 1)
-                geo_copies[step].start()
-
-        for step in range(1, rows):
-            if (step // 2) & (step // 2 - 1):
-
-                @pl.when(order.apart(step))
-                def _():
-                    geo_copies[step].start()
+        later_sends(range(rows - 2, rows), row < 2)
 
     for copy in loads[1]:
         copy.wait()
@@ -393,7 +404,7 @@
         (4 * face_q, 4 * QP),
         lambda r, c: (r == (c % QP) * 4 + c // QP) & (c % QP < face_q),
     )
-    at = tests_at[1] + 3 * unit * len(groups[1])
+    at = tests_at[2]
     tests[:, at : at + 4 * QP] = (-dot(flat, place, 0, 0)).astype(BF16)
 
     lame = material[0:1, :]
@@ -498,7 +509,7 @@
                 shear = [a1 * own[6 + i] + b1 * met[6 + i] for i in range(3)]
                 force = [a2 * own[i] + b2 * met[i] for i in range(6)]
                 results = normal_flux(press, shear, force, n)
-                to = flux_at[1] + 3 * unit * len(groups[1]) + f * QP + part * 16
+                to = flux_at[2] + f * QP + part * 16
                 for m in range(9):
                     total = results[m] + pen * (own[m] - met[m])
                     fluxes[m, to : to + 16, cut] = total.astype(BF16)
@@ -507,22 +518,22 @@
     volume(groups[0])
     for m in range(quantities):
         out[m] = contract(0, m)
-    volume(groups[1])
     whole = pool.at[pl.ds(0, cols - 1)]
     pltpu.make_async_copy(whole, whole, face_recv).wait()
-    received = pool[...].reshape(cols * slots, quantities * QP)
-    gathered[...] = gathered[...] + dot(received, far[...], 0, 0)
+    received = pool[...].reshape(cols * slots, wire)
+    received = dot(narrow, received, 1, 1).astype(BF16)
+    gathered[...] = gathered[...] + dot(received, far[...])
     for f in range(4):
         surface_face(f)
     for m in range(quantities):
-        out[m] = out[m] + contract(1, m)
-    volume(groups[2])
+        out[m] = out[m] + contract(2, m)
+    volume(groups[1])
     whole = metric.at[pl.ds(0, rows - 1)]
     pltpu.make_async_copy(whole, whole, geo_send).wait()
     whole = outgoing.at[pl.ds(0, cols - 1)]
     pltpu.make_async_copy(whole, whole, face_send).wait()
     for m in range(quantities):
-        out[m] = state[m] + factor * (out[m] + contract(2, m))
+        out[m] = state[m] + factor * (out[m] + contract(1, m))
 
 
 def normal_flux(press, shear, force, n):
@@ -561,6 +572,7 @@
     vol_q = vol_eval.shape[1]
     local_q = geometry.shape[1]
     total = 3 * vol_q + 4 * QP
+    wire = (quantities * (face_eval.shape[2] + 1) + 127) // 128 * 128
     tests_at = tiles(vol_q, max(local_q, 16))[3]
     operands = [
         state,
@@ -581,8 +593,8 @@
         pltpu.VMEM((quantities, basis, elems), BF16),
         pltpu.VMEM((quantities, 4 * QP, elems), F32),
         pltpu.VMEM((quantities * QP, 4 * elems), BF16),
-        pltpu.VMEM((cols, slots, quantities * QP), BF16),
-        pltpu.VMEM((cols, slots, quantities * QP), BF16),
+        pltpu.VMEM((cols, slots, wire), BF16),
+        pltpu.VMEM((cols, slots, wire), BF16),
         pltpu.VMEM((quantities * QP, 4 * elems), F32),
         pltpu.VMEM((quantities, vol_q, elems), F32),
         pltpu.VMEM((quantities, total, elems), BF16),

time: 12.9 us -> 13.1 us (1.016)
  Pallas kernels: 12 us -> 12.2 us
    pallas_call x1, Pallas kernels: 12 us -> 12.2 us  [per_device(): pl.pallas_call(functools.partial(kernel, rows, cols), out_shape=jax.Shape...]
where the time goes in v3:
time: 13.1 us; the launch traced here: 13 us
  Pallas kernels  12.2 us (93%)
  local copies, waits for them, and re-layouts  0.74 us (6%)
    pallas_call x1, Pallas kernels, per_device(): pl.pallas_call(functools.partial(kernel, rows, cols), out_shape=jax.Shape...  12.2 us
    unnamed x1, local copies, waits for them, and re-layouts  0.74 us

profile of v3, /device:TPU:0, one launch (start us, length us, event | category | flops | bytes accessed | tf_op | source)
XLA Modules:
  0.0 13.0 jit_solution(2622110262312859985)
XLA Ops:
  0.0 12.2 %shard_map.109 = f32[9,35,256]{2,1,0:T(8,128)S(1)} custom-call(f32[9,35,256]{2,1,0:T(8,128)} %state_in.1, bf16[9,16,2048]{2,1,0:T(8,128)(2,1)} %geometry.1, f32[4,256]{1,0:T(4,128)} %material_in.1, s32[4,4,256]{2,1,0:T(4,128)} %neighbours_in.1, s32[1,4,64]{2,1,0:T(4,128)} %send_in.1, f32[35,128]{1,0:T(8,128)} %vol_eval_in.1, ...), custom_call_target="tpu_custom_call" | custom-call | tf_op jit(solution)/shard_map/pallas_call | solution.py:616
  12.2 0.7 %copy.13 = f32[9,35,256]{2,1,0:T(8,128)} copy(f32[9,35,256]{2,1,0:T(8,128)S(1)} %shard_map.109) | data formatting | bytes 645120

commit v4 on v3

--- a/solution.py
+++ b/solution.py
@@ -109,6 +109,7 @@
     tests,
     normal_rows,
     area_rows,
+    own_flux,
     pick,
     far,
     load_sem,
@@ -278,6 +279,20 @@
     )
     for copy in loads[0]:
         copy.wait()
+    listed = send_faces[0]
+    listed_face = listed // elems
+    listed_elem = listed - listed_face * elems
+    face_col = dot(same, listed_face.astype(F32).astype(BF16), 1, 1)
+    elem_col = dot(same, listed_elem.astype(F32).astype(BF16), 1, 1)
+    listed_col = (face_col * float(elems) + elem_col).astype(jnp.int32)
+    face_ids = lax.broadcasted_iota(jnp.int32, (slots, 4 * elems), 1)
+    send_pick = jnp.concatenate(
+        [
+            jnp.where(face_ids == listed_col[:, p : p + 1], 1.0, 0.0).astype(BF16)
+            for p in range(cols)
+        ],
+        axis=0,
+    )
     flat = face_eval[...].reshape(4 * face_q, basis).astype(BF16)
     face_basis = dot(turning, flat).astype(BF16)
     for m in range(quantities):
@@ -307,7 +322,7 @@
             turned[m * QP : (m + 1) * QP, f * elems : (f + 1) * elems] = chosen.astype(BF16)
 
     if ordered:
-        later_sends(range(1, rows - 2))
+        later_sends(range(1, rows - 2), (row >= 2) | (col == 0))
         later_sends(range(rows - 2, rows), row >= 2)
         for step in range(1, rows):
             if (step // 2) & (step // 2 - 1):
@@ -316,20 +331,6 @@
                 def _():
                     geo_copies[step].start()
 
-    listed = send_faces[0]
-    listed_face = listed // elems
-    listed_elem = listed - listed_face * elems
-    face_col = dot(same, listed_face.astype(F32).astype(BF16), 1, 1)
-    elem_col = dot(same, listed_elem.astype(F32).astype(BF16), 1, 1)
-    listed_col = (face_col * float(elems) + elem_col).astype(jnp.int32)
-    face_ids = lax.broadcasted_iota(jnp.int32, (slots, 4 * elems), 1)
-    send_pick = jnp.concatenate(
-        [
-            jnp.where(face_ids == listed_col[:, p : p + 1], 1.0, 0.0).astype(BF16)
-            for p in range(cols)
-        ],
-        axis=0,
-    )
     listed_traces = dot(send_pick, turned[...], 1, 1).astype(BF16)
     listed_traces = dot(listed_traces, narrow).astype(BF16)
     for p in range(cols):
@@ -346,6 +347,7 @@
             face_copies[step - 1].start()
 
     if ordered:
+        later_sends(range(1, rows - 2), (row < 2) & (col > 0))
         later_sends(range(rows - 2, rows), row < 2)
 
     for copy in loads[1]:
@@ -473,9 +475,35 @@
         far[:, f * elems : (f + 1) * elems] = jnp.where(pool_ids == wanted, 1.0, 0.0).astype(BF16)
     own_speed = jnp.sqrt((lame + 2.0 * rigid) * light)
 
+    def face_parts(f):
+        for half in range(elems // 128):
+            for part in range(QP // 16):
+                yield slice(half * 128, (half + 1) * 128), f * QP + part * 16, part * 16
+
+    def own_face(f):
+        free = jnp.where(kind[f : f + 1] == 2, 1.0, 0.0)
+        for cut, at, part in face_parts(f):
+            a0, a1, a2 = -0.5 * lame[:, cut], -0.5 * rigid[:, cut], -0.5 * light[:, cut]
+            n = [normal_rows[i, at : at + 16, cut] for i in range(3)]
+            own = [traces[m, at : at + 16, cut] for m in range(9)]
+            results = normal_flux(
+                [a0 * own[6 + i] for i in range(3)],
+                [a1 * own[6 + i] for i in range(3)],
+                [a2 * own[i] for i in range(6)],
+                n,
+            )
+            left = f * elems + cut.start
+            for m in range(9):
+                own_flux[m, at : at + 16, cut] = results[m]
+                top = m * QP + part
+                part_own = free[:, cut] * own[m]
+                value = gathered[top : top + 16, left : left + 128]
+                gathered[top : top + 16, left : left + 128] = (
+                    value - part_own if m < 6 else value + part_own
+                )
+
     def surface_face(f):
         lanes = slice(f * elems, (f + 1) * elems)
-        free = jnp.where(kind[f : f + 1] == 2, 1.0, 0.0)
         edge = jnp.where(kind[f : f + 1] >= 2, 1.0, 0.0)
         other = []
         for i in range(3):
@@ -488,33 +516,27 @@
             )
         speed = jnp.sqrt((other[0] + 2.0 * other[1]) * other[2])
         penalty_scale = 0.5 * jnp.maximum(own_speed, speed)
-        for half in range(elems // 128):
-            cut = slice(half * 128, (half + 1) * 128)
-            a0, a1, a2 = -0.5 * lame[:, cut], -0.5 * rigid[:, cut], -0.5 * light[:, cut]
+        for cut, at, part in face_parts(f):
             b0, b1, b2 = -0.5 * other[0][:, cut], -0.5 * other[1][:, cut], -0.5 * other[2][:, cut]
-            mirror = free[:, cut]
-            for part in range(QP // 16):
-                at = f * QP + part * 16
-                n = [normal_rows[i, at : at + 16, cut] for i in range(3)]
-                pen = penalty_scale[:, cut] * area_rows[at : at + 16, cut]
-                own = [traces[m, at : at + 16, cut] for m in range(9)]
-                met = []
-                for m in range(9):
-                    top = m * QP + part * 16
-                    left = f * elems + half * 128
-                    value = gathered[top : top + 16, left : left + 128]
-                    part_own = mirror * own[m]
-                    met.append(value - part_own if m < 6 else value + part_own)
-                press = [a0 * own[6 + i] + b0 * met[6 + i] for i in range(3)]
-                shear = [a1 * own[6 + i] + b1 * met[6 + i] for i in range(3)]
-                force = [a2 * own[i] + b2 * met[i] for i in range(6)]
-                results = normal_flux(press, shear, force, n)
-                to = flux_at[2] + f * QP + part * 16
-                for m in range(9):
-                    total = results[m] + pen * (own[m] - met[m])
-                    fluxes[m, to : to + 16, cut] = total.astype(BF16)
+            n = [normal_rows[i, at : at + 16, cut] for i in range(3)]
+            pen = penalty_scale[:, cut] * area_rows[at : at + 16, cut]
+            left = f * elems + cut.start
+            met = [gathered[m * QP + part : m * QP + part + 16, left : left + 128] for m in range(9)]
+            results = normal_flux(
+                [b0 * met[6 + i] for i in range(3)],
+                [b1 * met[6 + i] for i in range(3)],
+                [b2 * met[i] for i in range(6)],
+                n,
+            )
+            to = flux_at[2] + at
+            for m in range(9):
+                gap = traces[m, at : at + 16, cut] - met[m]
+                total = own_flux[m, at : at + 16, cut] + results[m] + pen * gap
+                fluxes[m, to : to + 16, cut] = total.astype(BF16)
 
     factor = material[3:4, :]
+    for f in range(4):
+        own_face(f)
     volume(groups[0])
     for m in range(quantities):
         out[m] = contract(0, m)
@@ -601,6 +623,7 @@
         pltpu.VMEM((basis, tests_at[-1]), BF16),
         pltpu.VMEM((3, 4 * QP, elems), F32),
         pltpu.VMEM((4 * QP, elems), F32),
+        pltpu.VMEM((quantities, 4 * QP, elems), F32),
         pltpu.VMEM((4 * elems, elems), BF16),
         pltpu.VMEM((cols * slots, 4 * elems), BF16),
         pltpu.SemaphoreType.DMA((2,)),

time: 13.1 us -> 12.8 us (0.977)
  Pallas kernels: 12.2 us -> 11.9 us
    pallas_call x1, Pallas kernels: 12.2 us -> 11.9 us  [per_device(): pl.pallas_call(functools.partial(kernel, rows, cols), out_shape=jax.Shape...]
where the time goes in v4:
time: 12.8 us; the launch traced here: 12.7 us
  Pallas kernels  11.9 us (93%)
  local copies, waits for them, and re-layouts  0.74 us (6%)
    pallas_call x1, Pallas kernels, per_device(): pl.pallas_call(functools.partial(kernel, rows, cols), out_shape=jax.Shape...  11.9 us
    unnamed x1, local copies, waits for them, and re-layouts  0.74 us

profile of v4, /device:TPU:0, one launch (start us, length us, event | category | flops | bytes accessed | tf_op | source)
XLA Modules:
  0.0 12.7 jit_solution(17624638876054890766)
XLA Ops:
  0.0 11.9 %shard_map.109 = f32[9,35,256]{2,1,0:T(8,128)S(1)} custom-call(f32[9,35,256]{2,1,0:T(8,128)} %state_in.1, bf16[9,16,2048]{2,1,0:T(8,128)(2,1)} %geometry.1, f32[4,256]{1,0:T(4,128)} %material_in.1, s32[4,4,256]{2,1,0:T(4,128)} %neighbours_in.1, s32[1,4,64]{2,1,0:T(4,128)} %send_in.1, f32[35,128]{1,0:T(8,128)} %vol_eval_in.1, ...), custom_call_target="tpu_custom_call" | custom-call | tf_op jit(solution)/shard_map/pallas_call | solution.py:639
  11.9 0.7 %copy.13 = f32[9,35,256]{2,1,0:T(8,128)} copy(f32[9,35,256]{2,1,0:T(8,128)S(1)} %shard_map.109) | data formatting | bytes 645120

commit v5 on v4

--- a/solution.py
+++ b/solution.py
@@ -240,11 +240,13 @@
                     device_id_type=MESH,
                 )
 
-        for step in range(1, rows):
-
-            @pl.when(order.earlier(step))
-            def _():
-                geo_copies[step].start()
+        far_first = sorted(range(1, rows), key=lambda step: (-(step // 2), step))
+        for core, steps in ((0, range(1, rows)), (1, far_first)):
+            for step in steps:
+
+                @pl.when(order.earlier(step) & (row % 2 == core))
+                def _():
+                    geo_copies[step].start()
 
         for step in range(1, cols):
 

time: 12.8 us -> 12.7 us (level)
  the two profiles are of different devices: /device:TPU:0 before, /device:TPU:1 now
where the time goes in v5:
time: 12.7 us; the launch traced here: 12.6 us
  Pallas kernels  11.8 us (93%)
  local copies, waits for them, and re-layouts  0.74 us (6%)
    pallas_call x1, Pallas kernels, per_device(): pl.pallas_call(functools.partial(kernel, rows, cols), out_shape=jax.Shape...  11.8 us
    unnamed x1, local copies, waits for them, and re-layouts  0.74 us

profile of v5, /device:TPU:1, one launch (start us, length us, event | category | flops | bytes accessed | tf_op | source)
XLA Modules:
  0.0 12.6 jit_solution(11388418889549771885)
XLA Ops:
  0.0 11.8 %shard_map.109 = f32[9,35,256]{2,1,0:T(8,128)S(1)} custom-call(f32[9,35,256]{2,1,0:T(8,128)} %state_in.1, bf16[9,16,2048]{2,1,0:T(8,128)(2,1)} %geometry.1, f32[4,256]{1,0:T(4,128)} %material_in.1, s32[4,4,256]{2,1,0:T(4,128)} %neighbours_in.1, s32[1,4,64]{2,1,0:T(4,128)} %send_in.1, f32[35,128]{1,0:T(8,128)} %vol_eval_in.1, ...), custom_call_target="tpu_custom_call" | custom-call | tf_op jit(solution)/shard_map/pallas_call | solution.py:641
  11.8 0.7 %copy.13 = f32[9,35,256]{2,1,0:T(8,128)} copy(f32[9,35,256]{2,1,0:T(8,128)S(1)} %shard_map.109) | data formatting | bytes 645120

commit v6 on v5

--- a/solution.py
+++ b/solution.py
@@ -342,7 +342,7 @@
     for step in range(1, cols):
         if ordered:
 
-            @pl.when(col + step >= cols)
+            @pl.when((col + step >= cols) & (row % 2 == 0))
             def _():
                 face_copies[step - 1].start()
         else:
@@ -358,6 +358,13 @@
     vol_basis = dot(same_q, vol_eval[...].astype(BF16), 1, 1).astype(BF16)
     for m in range(quantities):
         points[m] = dot(vol_basis, state_low[m])
+
+    if ordered:
+        for step in range(1, cols):
+
+            @pl.when((col + step >= cols) & (row % 2 == 1))
+            def _():
+                face_copies[step - 1].start()
 
     if ordered:
         for step in range(1, cols):

time: 12.7 us -> 12.7 us (level)
  no operation moved by 1% of the time
where the time goes in v6:
time: 12.7 us; the launch traced here: 12.6 us
  Pallas kernels  11.8 us (93%)
  local copies, waits for them, and re-layouts  0.74 us (6%)
    pallas_call x1, Pallas kernels, per_device(): pl.pallas_call(functools.partial(kernel, rows, cols), out_shape=jax.Shape...  11.8 us
    unnamed x1, local copies, waits for them, and re-layouts  0.74 us

profile of v6, /device:TPU:1, one launch (start us, length us, event | category | flops | bytes accessed | tf_op | source)
XLA Modules:
  0.0 12.6 jit_solution(12060896712626516420)
XLA Ops:
  0.0 11.8 %shard_map.109 = f32[9,35,256]{2,1,0:T(8,128)S(1)} custom-call(f32[9,35,256]{2,1,0:T(8,128)} %state_in.1, bf16[9,16,2048]{2,1,0:T(8,128)(2,1)} %geometry.1, f32[4,256]{1,0:T(4,128)} %material_in.1, s32[4,4,256]{2,1,0:T(4,128)} %neighbours_in.1, s32[1,4,64]{2,1,0:T(4,128)} %send_in.1, f32[35,128]{1,0:T(8,128)} %vol_eval_in.1, ...), custom_call_target="tpu_custom_call" | custom-call | tf_op jit(solution)/shard_map/pallas_call | solution.py:648
  11.8 0.7 %copy.13 = f32[9,35,256]{2,1,0:T(8,128)} copy(f32[9,35,256]{2,1,0:T(8,128)S(1)} %shard_map.109) | data formatting | bytes 645120
